TPU v7x, 32 devices: a whole 2x2x4 slice. The times are simulated.
32 devices in a mesh: ctx: 4 (over y, x), fsdp: 8 (over z, core).
Axes of the slice: x: 2, y: 2, z: 4, core: 2. Of those that a mesh axis runs over, the one named last changes fastest.
Arguments:
- query_a: bfloat16 [8, 512, 2048], P('fsdp', 'ctx'), may hold values from -64 to 64
- key_a: bfloat16 [8, 512, 256], P('fsdp', 'ctx'), may hold values from -8 to 8
- value_a: bfloat16 [8, 512, 256], P('fsdp', 'ctx'), may hold values from -6 to 6
- resid_in: bfloat16 [8, 512, 1440], P('fsdp', 'ctx'), may hold values from -6 to 6
- doc_lengths: int32 [8, 6], P('fsdp'), may hold values from 1 to 384, 512 in all within a row
- w_out: bfloat16 [2048, 1440], P('fsdp'), may hold values from -0.125 to 0.125
- w_qkv: bfloat16 [1440, 2560], P('fsdp'), may hold values from -8 to 8
- grad_out: bfloat16 [8, 512, 2048], P('fsdp', 'ctx'), may hold values from -6 to 6
- grad_resid: bfloat16 [8, 512, 1440], P('fsdp', 'ctx'), may hold values from -8 to 8
Outputs:
- banded_out: bfloat16 [8, 512, 2048], P('fsdp', 'ctx')
- grad_input: bfloat16 [8, 512, 1440], P('fsdp', 'ctx')
- grad_query: bfloat16 [8, 512, 2048], P('fsdp', 'ctx')
- grad_key: bfloat16 [8, 512, 256], P('fsdp', 'ctx')
- grad_value: bfloat16 [8, 512, 256], P('fsdp', 'ctx')
- grad_w_out: float32 [2048, 1440], P('fsdp')
- grad_w_qkv: float32 [1440, 2560], P('fsdp')
Inputs may be any that keep to these rules, and one draw needn't show every extreme that they name: `doc_lengths`: the lengths of a sequence sum to 512, and one document has 384 positions.
All inputs are finite; a program needn't handle non-finite values.
Results may differ from a plain program's by a relative error of at most 0.03.
Values may be sent and summed in bfloat16 or wider, within the bound.
A program may use at most 128 MiB of HBM per device.

v0:
```python
import math

import jax
import jax.numpy as jnp
from jax import lax
from jax.sharding import PartitionSpec as P

H = 32
KV = 4
DH = 64
BAND = 128


MASKED = -1e30
EPSILON = 1e-05


def partner_2(value, axis, stride):
    mask = 2**stride
    pairs = [(source, source ^ mask) for source in range(lax.axis_size(axis))]
    return lax.ppermute(value, axis, pairs)


def from_behind(value, axis, steps):
    count = lax.axis_size(axis)
    leading, last = (max(0, -steps), min(count, count - steps))
    return lax.ppermute(value, axis, [(source, source + steps) for source in range(leading, last)])


def doc_tables(lengths, seq_len):
    ends = jnp.cumsum(lengths)
    places = jnp.arange(seq_len, dtype=jnp.int32)
    before = places[:, None] >= ends[None, :]
    documents = jnp.sum(before.astype(jnp.int32), axis=1)
    doc_starts = jnp.sum(jnp.where(before, lengths[None, :], 0), axis=1)
    return (documents, doc_starts)


def split_heads(rows):
    return rows.reshape(rows.shape[0], KV, H // KV, DH)


def masked_softmax(scores, allowed):
    row_max = jnp.max(scores, axis=-1, keepdims=True)
    log_total = row_max + jnp.log(
        jnp.sum(jnp.where(allowed, jnp.exp(scores - row_max), 0.0), axis=-1, keepdims=True)
    )
    return jnp.where(allowed, jnp.exp(scores - log_total), 0.0)


def full_scores(query_h, first_row, keys, documents, block_start, block_size):
    row_count = query_h.shape[0]
    key_block = lax.dynamic_slice_in_dim(keys, block_start, block_size).reshape(block_size, KV, DH)
    scores = jnp.einsum(
        "ikgd,jkd->kgij", query_h, key_block, preferred_element_type=jnp.float32
    ) * DH ** (-0.5)
    places = first_row + jnp.arange(row_count, dtype=jnp.int32)
    columns = block_start + jnp.arange(block_size, dtype=jnp.int32)
    row_docs = lax.dynamic_slice_in_dim(documents, first_row, row_count)
    col_docs = lax.dynamic_slice_in_dim(documents, block_start, block_size)
    allowed = (row_docs[:, None] == col_docs[None, :]) & (columns[None, :] <= places[:, None])
    return (jnp.where(allowed, scores, MASKED), allowed, key_block)


def block_range(first_row, row_count, doc_starts, block_size):
    lowest = doc_starts[first_row] // block_size
    highest = (first_row + row_count + block_size - 1) // block_size
    return (lowest, highest)


def full_forward(query, first_row, keys, values, documents, doc_starts, block_size):
    row_count = query.shape[0]
    group = H // KV
    query_h = split_heads(query)
    lowest, highest = block_range(first_row, row_count, doc_starts, block_size)

    def gather_stats(block_id, carry):
        row_max, summed = carry
        scores, allowed, unused = full_scores(
            query_h, first_row, keys, documents, block_id * block_size, block_size
        )
        fresh_max = jnp.maximum(row_max, jnp.max(scores, axis=-1))
        kept = jnp.where(allowed, jnp.exp(scores - fresh_max[..., None]), 0.0)
        return (fresh_max, summed * jnp.exp(row_max - fresh_max) + jnp.sum(kept, axis=-1))

    start_max = jnp.full((KV, group, row_count), MASKED, jnp.float32)
    row_max, summed = lax.fori_loop(
        lowest, highest, gather_stats, (start_max, jnp.zeros_like(start_max))
    )
    log_total = row_max + jnp.log(summed)

    def add_values(block_id, output):
        block_start = block_id * block_size
        scores, allowed, unused = full_scores(
            query_h, first_row, keys, documents, block_start, block_size
        )
        weights = jnp.where(allowed, jnp.exp(scores - log_total[..., None]), 0.0).astype(
            jnp.bfloat16
        )
        value_block = lax.dynamic_slice_in_dim(values, block_start, block_size).reshape(
            block_size, KV, DH
        )
        return output + jnp.einsum(
            "kgij,jkd->ikgd", weights, value_block, preferred_element_type=jnp.float32
        )

    output = lax.fori_loop(
        lowest, highest, add_values, jnp.zeros((row_count, KV, group, DH), jnp.float32)
    )
    return (output.astype(jnp.bfloat16).reshape(row_count, H * DH), log_total)


def full_backward(
    query,
    first_row,
    keys,
    values,
    output,
    grad,
    log_total,
    documents,
    doc_starts,
    block_size,
    key_sums,
    value_sums,
):
    row_count = query.shape[0]
    group = H // KV
    query_h = split_heads(query)
    grad_h = split_heads(grad)
    correction = jnp.einsum(
        "ikgd,ikgd->kgi", grad_h, split_heads(output), preferred_element_type=jnp.float32
    )
    lowest, highest = block_range(first_row, row_count, doc_starts, block_size)

    def accumulate(block_id, carry):
        grad_q, key_acc, value_acc = carry
        block_start = block_id * block_size
        scores, allowed, key_block = full_scores(
            query_h, first_row, keys, documents, block_start, block_size
        )
        weights = jnp.where(allowed, jnp.exp(scores - log_total[..., None]), 0.0)
        weights_bf = weights.astype(jnp.bfloat16)
        value_block = lax.dynamic_slice_in_dim(values, block_start, block_size).reshape(
            block_size, KV, DH
        )
        grad_weights = jnp.einsum(
            "ikgd,jkd->kgij", grad_h, value_block, preferred_element_type=jnp.float32
        )
        grad_scores = (weights * (grad_weights - correction[..., None])).astype(jnp.bfloat16)
        grad_q = grad_q + jnp.einsum(
            "kgij,jkd->ikgd", grad_scores, key_block, preferred_element_type=jnp.float32
        )
        key_term = jnp.einsum(
            "kgij,ikgd->jkd", grad_scores, query_h, preferred_element_type=jnp.float32
        )
        value_term = jnp.einsum(
            "kgij,ikgd->jkd", weights_bf, grad_h, preferred_element_type=jnp.float32
        )
        key_old = lax.dynamic_slice_in_dim(key_acc, block_start, block_size)
        value_old = lax.dynamic_slice_in_dim(value_acc, block_start, block_size)
        key_acc = lax.dynamic_update_slice_in_dim(
            key_acc, key_old + key_term.reshape(block_size, KV * DH), block_start, 0
        )
        value_acc = lax.dynamic_update_slice_in_dim(
            value_acc, value_old + value_term.reshape(block_size, KV * DH), block_start, 0
        )
        return (grad_q, key_acc, value_acc)

    start = (jnp.zeros((row_count, KV, group, DH), jnp.float32), key_sums, value_sums)
    grad_q, key_sums, value_sums = lax.fori_loop(lowest, highest, accumulate, start)
    grad_q = (grad_q * DH ** (-0.5)).astype(jnp.bfloat16).reshape(row_count, H * DH)
    return (grad_q, key_sums, value_sums)


def band_scores(query_h, keys_ext, doc_ext, block_start, block_size, band_len):
    width = band_len + block_size
    key_block = keys_ext.reshape(width, KV, DH)
    scores = jnp.einsum(
        "ikgd,jkd->kgij", query_h, key_block, preferred_element_type=jnp.float32
    ) * DH ** (-0.5)
    places = block_start + band_len + jnp.arange(block_size, dtype=jnp.int32)
    columns = block_start + jnp.arange(width, dtype=jnp.int32)
    row_docs = lax.dynamic_slice_in_dim(doc_ext, block_start + band_len, block_size)
    allowed = (row_docs[:, None] == doc_ext[None, :]) & (columns[None, :] <= places[:, None])
    allowed = allowed & (columns[None, :] > places[:, None] - band_len)
    return (jnp.where(allowed, scores, MASKED), allowed, query_h, key_block)


def band_forward(query, keys_ext, values_ext, doc_ext, band_len, block_size):
    row_count = query.shape[0]
    width = band_len + block_size
    query_h = split_heads(query)

    def one_block(block_id, output):
        block_start = block_id * block_size
        scores, allowed, unused, unused_keys = band_scores(
            query_h, keys_ext, doc_ext, block_start, block_size, band_len
        )
        weights = masked_softmax(scores, allowed).astype(jnp.bfloat16)
        value_block = values_ext.reshape(width, KV, DH)
        result = jnp.einsum(
            "kgij,jkd->ikgd", weights, value_block, preferred_element_type=jnp.float32
        )
        return result.astype(jnp.bfloat16)

    output = lax.fori_loop(
        0, row_count // block_size, one_block, jnp.zeros((row_count, KV, H // KV, DH), jnp.bfloat16)
    )
    return output.reshape(row_count, H * DH)


def band_backward(query, keys_ext, values_ext, doc_ext, output, grad, band_len, block_size):
    row_count = query.shape[0]
    width = band_len + block_size
    query_h = split_heads(query)
    grad_h = split_heads(grad)
    out_h = split_heads(output)

    def one_block(block_id, carry):
        grad_q, key_acc, value_acc = carry
        block_start = block_id * block_size
        scores, allowed, query_block, key_block = band_scores(
            query_h, keys_ext, doc_ext, block_start, block_size, band_len
        )
        weights = masked_softmax(scores, allowed)
        weights_bf = weights.astype(jnp.bfloat16)
        value_block = values_ext.reshape(width, KV, DH)
        correction = jnp.einsum("ikgd,ikgd->kgi", grad_h, out_h, preferred_element_type=jnp.float32)
        grad_weights = jnp.einsum(
            "ikgd,jkd->kgij", grad_h, value_block, preferred_element_type=jnp.float32
        )
        grad_scores = (weights * (grad_weights - correction[..., None])).astype(jnp.bfloat16)
        query_term = jnp.einsum(
            "kgij,jkd->ikgd", grad_scores, key_block, preferred_element_type=jnp.float32
        )
        grad_q = (query_term * DH ** (-0.5)).astype(jnp.bfloat16)
        key_term = jnp.einsum(
            "kgij,ikgd->jkd", grad_scores, query_block, preferred_element_type=jnp.float32
        )
        value_term = jnp.einsum(
            "kgij,ikgd->jkd", weights_bf, grad_h, preferred_element_type=jnp.float32
        )
        key_old = key_acc
        value_old = value_acc
        key_acc = key_old + key_term.reshape(width, KV * DH)
        value_acc = value_old + value_term.reshape(width, KV * DH)
        return (grad_q, key_acc, value_acc)

    start = (
        jnp.zeros((row_count, KV, H // KV, DH), jnp.bfloat16),
        jnp.zeros((band_len + row_count, KV * DH), jnp.float32),
        jnp.zeros((band_len + row_count, KV * DH), jnp.float32),
    )
    grad_q, key_acc, value_acc = lax.fori_loop(0, row_count // block_size, one_block, start)
    return (grad_q.reshape(row_count, H * DH), key_acc, value_acc)


def per_device(query_a, key_a, value_a, resid_in, doc_lengths, w_out, w_qkv, grad_out, grad_resid):
    ctx_count = lax.axis_size("ctx")
    ctx_index = lax.axis_index("ctx")
    local_rows = query_a.shape[1]
    seq_len = local_rows * ctx_count
    band_len = BAND
    half_rows = local_rows // 2
    key_block_size = math.gcd(seq_len, 256)
    row_block_size = math.gcd(local_rows, 256)
    first_row = ctx_index * local_rows
    documents, doc_starts = doc_tables(doc_lengths[0], seq_len)
    w_o, w_b = (
        lax.all_gather(w_out, "fsdp", axis=0, tiled=True),
        lax.all_gather(w_qkv, "fsdp", axis=0, tiled=True),
    )
    keys, values = (
        lax.all_gather(key_a[0], "ctx", axis=0, tiled=True),
        lax.all_gather(value_a[0], "ctx", axis=0, tiled=True),
    )
    query = query_a[0]
    swap_bit = ctx_count.bit_length() - 2
    partner = jnp.where(
        ctx_index < ctx_count // 2, ctx_index + ctx_count // 2, ctx_index - ctx_count // 2
    )
    moved = partner_2(query[half_rows:], "ctx", swap_bit)
    groups = ((query[:half_rows], first_row), (moved, partner * local_rows + half_rows))
    forwards = [
        full_forward(rows, start, keys, values, documents, doc_starts, key_block_size)
        for rows, start in groups
    ]
    returned = partner_2(forwards[1][0], "ctx", swap_bit)
    attended = jnp.concatenate([forwards[0][0], returned], axis=0)
    resid_mid = (
        resid_in[0].astype(jnp.float32) + jnp.dot(attended, w_o, preferred_element_type=jnp.float32)
    ).astype(jnp.bfloat16)
    resid_f = resid_mid.astype(jnp.float32)
    inverse_rms = lax.rsqrt(jnp.mean(resid_f * resid_f, axis=-1, keepdims=True) + EPSILON)
    normed = resid_f * inverse_rms
    normed_bf = normed.astype(jnp.bfloat16)
    projected = jnp.dot(normed_bf, w_b, preferred_element_type=jnp.float32).astype(jnp.bfloat16)
    query_b = projected[:, : H * DH]
    key_b = projected[:, H * DH : H * DH + KV * DH]
    value_b = projected[:, H * DH + KV * DH :]
    tail_keys, tail_values = from_behind((key_b, value_b), "ctx", 1)
    keys_ext = jnp.concatenate([tail_keys, key_b], axis=0)
    values_ext = jnp.concatenate([tail_values, value_b], axis=0)
    doc_pad = jnp.concatenate([jnp.full((band_len,), -1, jnp.int32), documents])
    doc_ext = lax.dynamic_slice_in_dim(doc_pad, first_row, band_len + local_rows)
    banded = band_forward(query_b, keys_ext, values_ext, doc_ext, band_len, row_block_size)
    grad_qb, key_ext_grad, value_ext_grad = band_backward(
        query_b, keys_ext, values_ext, doc_ext, banded, grad_out[0], band_len, row_block_size
    )
    head_keys, head_values = (
        from_behind(key_ext_grad[:band_len].astype(jnp.bfloat16), "ctx", -1).astype(jnp.float32),
        from_behind(value_ext_grad[:band_len].astype(jnp.bfloat16), "ctx", -1).astype(jnp.float32),
    )
    grad_kb = key_ext_grad[band_len:].at[local_rows - band_len :].add(head_keys)
    grad_vb = value_ext_grad[band_len:].at[local_rows - band_len :].add(head_values)
    grad_kb = (grad_kb * DH ** (-0.5)).astype(jnp.bfloat16)
    grad_vb = grad_vb.astype(jnp.bfloat16)
    grad_proj = jnp.concatenate([grad_qb, grad_kb, grad_vb], axis=1)
    piece = normed_bf
    qkv_share = lax.psum_scatter(
        jnp.einsum("tf,tc->fc", piece, grad_proj, preferred_element_type=jnp.float32).astype(
            jnp.bfloat16
        ),
        "fsdp",
        scatter_dimension=0,
        tiled=True,
    )
    grad_normed = jnp.dot(grad_proj, w_b.T, preferred_element_type=jnp.float32)
    middle = jnp.mean(grad_normed * normed, axis=-1, keepdims=True)
    grad_mid = (
        grad_resid[0].astype(jnp.float32) + inverse_rms * (grad_normed - normed * middle)
    ).astype(jnp.bfloat16)
    grad_attended = jnp.dot(grad_mid, w_o.T, preferred_element_type=jnp.float32).astype(
        jnp.bfloat16
    )
    piece = attended
    out_share = lax.psum_scatter(
        jnp.einsum("tf,tc->fc", piece, grad_mid, preferred_element_type=jnp.float32).astype(
            jnp.bfloat16
        ),
        "fsdp",
        scatter_dimension=0,
        tiled=True,
    )
    moved_grad = partner_2(grad_attended[half_rows:], "ctx", swap_bit)
    grad_groups = (grad_attended[:half_rows], moved_grad)
    key_sums = jnp.zeros((seq_len, KV * DH), jnp.float32)
    value_sums = jnp.zeros((seq_len, KV * DH), jnp.float32)
    query_grads = []
    for (rows, start), (output, log_total), grad in zip(groups, forwards, grad_groups):
        grad_q, key_sums, value_sums = full_backward(
            rows,
            start,
            keys,
            values,
            output,
            grad,
            log_total,
            documents,
            doc_starts,
            key_block_size,
            key_sums,
            value_sums,
        )
        query_grads.append(grad_q)
    back_grad = partner_2(query_grads[1], "ctx", swap_bit)
    grad_query = jnp.concatenate([query_grads[0], back_grad], axis=0)
    own_keys, own_values = (
        lax.psum_scatter(
            key_sums.astype(jnp.bfloat16), "ctx", scatter_dimension=0, tiled=True
        ).astype(jnp.float32),
        lax.psum_scatter(
            value_sums.astype(jnp.bfloat16), "ctx", scatter_dimension=0, tiled=True
        ).astype(jnp.float32),
    )
    grad_key = (own_keys * DH ** (-0.5)).astype(jnp.bfloat16)
    grad_value = own_values.astype(jnp.bfloat16)
    grad_w_out, grad_w_qkv = (
        lax.psum(out_share, "ctx").astype(jnp.float32),
        lax.psum(qkv_share, "ctx").astype(jnp.float32),
    )
    return (
        banded[None],
        grad_mid[None],
        grad_query[None],
        grad_key[None],
        grad_value[None],
        grad_w_out,
        grad_w_qkv,
    )


def solution(mesh):
    in_specs = (
        P("fsdp", "ctx", None),
        P("fsdp", "ctx", None),
        P("fsdp", "ctx", None),
        P("fsdp", "ctx", None),
        P("fsdp", None),
        P("fsdp", None),
        P("fsdp", None),
        P("fsdp", "ctx", None),
        P("fsdp", "ctx", None),
    )
    out_specs = (
        P("fsdp", "ctx", None),
        P("fsdp", "ctx", None),
        P("fsdp", "ctx", None),
        P("fsdp", "ctx", None),
        P("fsdp", "ctx", None),
        P("fsdp", None),
        P("fsdp", None),
    )
    return jax.shard_map(
        per_device, mesh=mesh, in_specs=in_specs, out_specs=out_specs, check_vma=False
    )
```

profile of v0, /device:TPU:0, one launch (start us, length us, event | category | flops | bytes accessed | tf_op | source)
XLA Modules:
  0.0 457.2 jit_solution(4518642787196685492)
XLA Ops:
  9.0 3.1 collective-permute-start
  18.6 9.2 %all-gather.1 = bf16[1,512,256]{1,2,0:T(8,128)(2,1)S(1)} all-gather(bf16[1,128,256]{1,2,0:T(8,128)(2,1)S(1)} %copy.117), channel_id=3, replica_groups=mesh['ctx'=4,'fsdp'=8] {'ctx'}, dimensions={1}, use_global_device_ids=true | all-gather | bytes 327680 | tf_op jit(solution)/shard_map/all_gather | solution.py:275
  30.0 9.8 %all-gather = bf16[1,512,256]{1,2,0:T(8,128)(2,1)S(1)} all-gather(bf16[1,128,256]{1,2,0:T(8,128)(2,1)S(1)} %copy.116), channel_id=2, replica_groups=mesh['ctx'=4,'fsdp'=8] {'ctx'}, dimensions={1}, use_global_device_ids=true | all-gather | bytes 327680 | tf_op jit(solution)/shard_map/all_gather | solution.py:276
  41.0 3.3 while.102
  45.4 6.8 %while.103 = (s32[]{:T(128)}, f32[64,4,8,64]{0,3,2,1:T(8,128)}, s32[]{:T(128)}, bf16[512,256]{0,1:T(8,128)(2,1)S(1)}, s32[64]{0:T(128)S(1)}, /*index=5*/s32[512]...) while((s32[]{:T(128)}, f32[64,4,8,64]{0,3,2,1:T(8,128)}, ...), condition=%wide.region_14.15_spmd, body=%wide.region_13.14_spmd.sunk | while | flops 137019712 | bytes 2144203 | solution.py:107
  45.6 3.2 fusion.177
  49.0 3.2 fusion.177
  56.9 8.1 %collective-permute-done.1 = bf16[64,2048]{0,1:T(8,128)(2,1)} collective-permute-done((bf16[64,2048]{0,1:T(8,128)(2,1)}, bf16[64,2048]{0,1:T(8,128)(2,1)}, u32[]{:S(2)}, u32[]{:S(2)}) %collective-permute-start.1) | collective-permute-done | bytes 262176 | tf_op jit(solution)/shard_map/ppermute | solution.py:21
  65.1 9.2 %all-gather.6.cloned.1.call-done = bf16[2048,1440]{0,1:T(8,128)(2,1)} async-done(((bf16[256,1440]{0,1:T(8,128)(2,1)}), bf16[2048,1440]{0,1:T(8,128)(2,1)}) %all-gather.6.cloned.1.call-update) | async-done | bytes 5898256 | tf_op jit(solution)/shard_map/all_gather | solution.py:271
  74.3 4.8 %multiply_reduce_fusion.3 = (f32[128]{0:T(128)S(1)}, f32[128,1440]{0,1:T(8,128)S(1)}) fusion(bf16[2048,1440]{0,1:T(8,128)(2,1)} %all-gather.6.cloned.1.call-done, bf16[64,2048]{0,1:T(8,128)(2,1)} %collective-permute-done.1, bf16[64,2048]{0,1:T(8,128)(2,1)} %bitcast.437, bf16[1,128,1440]{1,2,0:T(8,128)(2,1)} %param.32), kind=kOutput, calls=%fused_computation.127 | convolution fusion | flops 757129088 | bytes 7528960 | tf_op jit(solution)/shard_map/dot_general | solution.py:292
  79.1 70.0 %all-gather.8.cloned.1.call-done = bf16[8,180,2560]{2,1,0:T(8,128)(2,1)} async-done(((bf16[1,180,2560]{2,1,0:T(8,128)(2,1)}), bf16[8,180,2560]{2,1,0:T(8,128)(2,1)}) %all-gather.8.cloned.1.call-update) | async-done | bytes 7372816 | tf_op jit(solution)/shard_map/all_gather | solution.py:272
  149.1 7.0 %reshape.339 = bf16[1440,2560]{1,0:T(8,128)(2,1)} reshape(bf16[8,180,2560]{2,1,0:T(8,128)(2,1)} %all-gather.8.cloned.1.call-done) | data formatting | bytes 14745600
  156.2 4.4 convolution_convert_fusion.2
  161.2 4.0 collective-permute-start.2
  165.6 3.4 collective-permute-start.3
  186.8 3.9 collective-permute-done.5
  190.8 5.3 %multiply_reduce_fusion.2 = (f32[128]{0:T(128)S(1)}, f32[128,1440]{0,1:T(8,128)S(1)}) fusion(f32[128,1440]{0,1:T(8,128)S(1)} %get-tuple-element.1330, f32[128]{0:T(128)S(1)} %add_rsqrt_fusion, bf16[1440,2560]{1,0:T(8,128)(2,1)} %reshape.339, bf16[128,256]{0,1:T(8,128)(2,1)S(1)} %fusion.59, bf16[128,256]{0,1:T(8,128)(2,1)S(1)} %copy.134, ...), kind=kOutput, calls=%fused_computation.126 | convolution fusion | flops 946237312 | bytes 9503744 | tf_op jit(solution)/shard_map/dot_general | solution.py:329
  201.1 2.8 copy.179
  205.4 5.4 %convolution_convert_fusion.1 = bf16[2048,1440]{0,1:T(8,128)(2,1)} fusion(bf16[128,1440]{0,1:T(8,128)(2,1)S(1)} %fusion.57, bf16[64,2048]{0,1:T(8,128)(2,1)} %collective-permute-done.1, bf16[64,2048]{0,1:T(8,128)(2,1)S(1)} %bitcast.438), kind=kOutput, calls=%fused_computation.99 | convolution fusion | flops 758972416 | bytes 6791168 | tf_op jit(solution)/shard_map/tf,tc->fc/dot_general | solution.py:339
  212.0 4.1 while.104
  216.1 7.7 %collective-permute-start.6 = (bf16[64,2048]{1,0:T(8,128)(2,1)}, bf16[64,2048]{1,0:T(8,128)(2,1)S(1)}, u32[]{:S(2)}, u32[]{:S(2)}) collective-permute-start(bf16[64,2048]{1,0:T(8,128)(2,1)} %get-tuple-element.1321), channel_id=1, source_target_pairs={{0,16},{8,24},{16,0},{24,8},{1,17},{9,25},{17,1},{25,9},{2,18},{10... | collective-permute-start | bytes 786440 | tf_op jit(solution)/shard_map/ppermute | solution.py:21
  223.8 6.3 %convolution_convert_fusion = bf16[1440,2560]{1,0:T(8,128)(2,1)} fusion(bf16[128,256]{0,1:T(8,128)(2,1)S(1)} %copy-done.26, bf16[128,256]{0,1:T(8,128)(2,1)S(1)} %copy-done.24, bf16[128,2048]{0,1:T(8,128)(2,1)} %bitcast.442, f32[128,1440]{0,1:T(8,128)} %copy-done.10, f32[128]{0:T(128)S(1)} %copy-done.36), kind=kOutput, calls=%fused_computation.98 | convolution fusion | flops 949739520 | bytes 8765952 | tf_op jit(solution)/shard_map/tf,tc->fc/dot_general | solution.py:322
  232.1 2.2 bitcast_convert_fusion
  234.3 2.8 copy.185
  238.7 11.5 %while.105 = (s32[]{:T(128)}, f32[64,4,8,64]{0,3,2,1:T(8,128)S(1)}, f32[512,256]{0,1:T(8,128)}, f32[512,256]{0,1:T(8,128)}, s32[]{:T(128)}, /*index=5*/bf16[512,...) while((s32[]{:T(128)}, f32[64,4,8,64]{0,3,2,1:T(8,128)S(1)}, ...), condition=%wide.region_22.23_spmd, body=%wide.region_21.22_spmd.sunk | while | flops 340050240 | bytes 24041600 | solution.py:171
  252.1 94.5 %fusion = bf16[184,2560]{1,0:T(8,128)(2,1)S(1)} fusion(bf16[1440,2560]{1,0:T(8,128)(2,1)} %convolution_convert_fusion), kind=kCustom, calls=%all-reduce-scatter | all-reduce-scatter fusion | flops 3768321 | bytes 8315392
  349.2 5.8 %concatenate.30 = bf16[212,2560]{1,0:T(8,128)(2,1)} concatenate(bf16[28,2560]{1,0:T(8,128)(2,1)S(1)} %collective-permute-done.8, bf16[184,2560]{1,0:T(8,128)(2,1)S(1)} %fusion), dimensions={0} | concatenate | bytes 2170880
  355.0 2.4 constant_dynamic-slice_fusion.10
  361.6 7.0 %collective-permute-done.7 = bf16[64,2048]{1,0:T(8,128)(2,1)S(1)} collective-permute-done((bf16[64,2048]{1,0:T(8,128)(2,1)S(1)}, bf16[64,2048]{1,0:T(8,128)(2,1)S(1)}, u32[]{:S(2)}, u32[]{:S(2)}) %collective-permute-start.7) | collective-permute-done | bytes 262176 | tf_op jit(solution)/shard_map/ppermute | solution.py:21
  370.9 51.7 %all-reduce.6.cloned.1.call-done = (bf16[256,1440]{0,1:T(8,128)(2,1)}, bf16[180,2560]{1,0:T(8,128)(2,1)}) async-done(((bf16[256,1440]{0,1:T(8,128)(2,1)}, bf16[180,2560]{1,0:T(8,128)(2,1)}), (bf16[256,1440]{0,1:T(8,128)(2,1)}, bf16[180,2560]{1,0:T(8,128)(2,1)})) %all-reduce.6.cloned.1.call-update) | async-done | bytes 1658896 | tf_op jit(solution)/shard_map/psum | solution.py:380
  422.6 2.4 convert_element_type.177
  426.5 23.9 %reduce-scatter.8.cloned.1.call-done = bf16[128,256]{1,0:T(8,128)(2,1)} async-done(((bf16[512,256]{1,0:T(8,128)(2,1)}), bf16[128,256]{1,0:T(8,128)(2,1)}) %reduce-scatter.8.cloned.1.call-update) | async-done | bytes 65552 | tf_op jit(solution)/shard_map/reduce_scatter | solution.py:373
  (280 shorter events, 75.1 us)
Async XLA Ops:
  7.2 11.1 %copy-start.29 = (bf16[1,128,256]{2,1,0:T(8,128)(2,1)S(1)}, bf16[1,128,256]{2,1,0:T(8,128)(2,1)}, u32[]{:S(2)}) copy-start(bf16[1,128,256]{2,1,0:T(8,128)(2,1)} %param.31) | copy-start | bytes 196612
  7.2 11.3 %copy-start.30 = (bf16[1,128,256]{2,1,0:T(8,128)(2,1)S(1)}, bf16[1,128,256]{2,1,0:T(8,128)(2,1)}, u32[]{:S(2)}) copy-start(bf16[1,128,256]{2,1,0:T(8,128)(2,1)} %param.30) | copy-start | bytes 196612
  7.2 67.1 %all-gather.6.cloned.1.call-start = ((), (), s32[]{:S(2)}) async-start(), calls=%async_computation.3 | async-start | bytes 6635520 | tf_op jit(solution)/shard_map/all_gather | solution.py:271
  7.9 141.2 %all-gather.8.cloned.1.call-start = ((), (), s32[]{:S(2)}) async-start(), calls=%async_computation.7 | async-start | bytes 8478720 | tf_op jit(solution)/shard_map/all_gather | solution.py:272
  9.0 30.8 %collective-permute-start = (bf16[64,2048]{1,0:T(8,128)(2,1)S(1)}, bf16[64,2048]{1,0:T(8,128)(2,1)S(1)}, u32[]{:S(2)}, u32[]{:S(2)}) collective-permute-start(bf16[64,2048]{1,0:T(8,128)(2,1)S(1)} %get-tuple-element.1324), channel_id=1, source_target_pairs={{0,16},{8,24},{16,0},{24,8},{1,17},{9,25},{17,1},{25,9},{2,18},{10... | collective-permute-start | bytes 786440 | tf_op jit(solution)/shard_map/ppermute | solution.py:21
  12.1 345.3 %reduce-scatter.10.cloned.1.call-start = ((), (), s32[]{:S(2)}) async-start(), calls=%async_computation.6 | async-start | bytes 6635520 | tf_op jit(solution)/shard_map/reduce_scatter | solution.py:338
  54.3 10.7 %collective-permute-start.1 = (bf16[64,2048]{0,1:T(8,128)(2,1)}, bf16[64,2048]{0,1:T(8,128)(2,1)}, u32[]{:S(2)}, u32[]{:S(2)}) collective-permute-start(bf16[64,2048]{0,1:T(8,128)(2,1)} %bitcast.80), channel_id=1, source_target_pairs={{0,16},{8,24},{16,0},{24,8},{1,17},{9,25},{17,1},{25,9},{2,18},{10... | collective-permute-start | bytes 786440 | tf_op jit(solution)/shard_map/ppermute | solution.py:21
  55.8 23.3 %copy-start.12 = (f32[64,4,8,64]{0,3,2,1:T(8,128)}, f32[64,4,8,64]{0,3,2,1:T(8,128)S(1)}, u32[]{:S(2)}) copy-start(f32[64,4,8,64]{0,3,2,1:T(8,128)S(1)} %get-tuple-element.869) | copy-start | bytes 1572868
  55.8 23.3 %copy-start.27 = (s32[64]{0:T(128)}, s32[64]{0:T(128)S(1)}, u32[]{:S(2)}) copy-start(s32[64]{0:T(128)S(1)} %get-tuple-element.2096) | copy-start | bytes 772
  55.8 23.3 %copy-start.33 = (f32[4,8,64]{2,1,0:T(8,128)}, f32[4,8,64]{2,1,0:T(8,128)S(1)}, u32[]{:S(2)}) copy-start(f32[4,8,64]{2,1,0:T(8,128)S(1)} %get-tuple-element.2103) | copy-start | bytes 24580
  79.1 117.1 %copy-start.10 = (f32[128,1440]{0,1:T(8,128)}, f32[128,1440]{0,1:T(8,128)S(1)}, u32[]{:S(2)}) copy-start(f32[128,1440]{0,1:T(8,128)S(1)} %get-tuple-element.1330) | copy-start | bytes 2211844
  79.1 111.7 %copy-start.35 = (f32[128]{0:T(128)}, f32[128]{0:T(128)S(1)}, u32[]{:S(2)}) copy-start(f32[128]{0:T(128)S(1)} %add_rsqrt_fusion) | copy-start | bytes 1540
  156.2 9.1 %copy-start.20 = (bf16[1,128,2048]{2,1,0:T(8,128)(2,1)S(1)}, bf16[1,128,2048]{2,1,0:T(8,128)(2,1)}, u32[]{:S(2)}) copy-start(bf16[1,128,2048]{2,1,0:T(8,128)(2,1)} %param.36) | copy-start | bytes 1572868
  161.2 8.1 %collective-permute-start.2 = (bf16[128,256]{1,0:T(8,128)(2,1)}, bf16[128,256]{1,0:T(8,128)(2,1)}, u32[]{:S(2)}, u32[]{:S(2)}) collective-permute-start(bf16[128,256]{1,0:T(8,128)(2,1)} %get-tuple-element.1320), channel_id=1, source_target_pairs={{0,8},{8,16},{16,24},{1,9},{9,17},{17,25},{2,10},{10,18},{18,26},{... | collective-permute-start | bytes 196616 | tf_op jit(solution)/shard_map/ppermute | solution.py:27
  165.6 5.0 %collective-permute-start.3 = (bf16[128,256]{1,0:T(8,128)(2,1)}, bf16[128,256]{1,0:T(8,128)(2,1)}, u32[]{:S(2)}, u32[]{:S(2)}) collective-permute-start(bf16[128,256]{1,0:T(8,128)(2,1)} %get-tuple-element.1319), channel_id=1, source_target_pairs={{0,8},{8,16},{16,24},{1,9},{9,17},{17,25},{2,10},{10,18},{18,26},{... | collective-permute-start | bytes 196616 | tf_op jit(solution)/shard_map/ppermute | solution.py:27
  180.1 6.5 %collective-permute-start.4 = (bf16[128,256]{1,0:T(8,128)(2,1)S(1)}, bf16[128,256]{1,0:T(8,128)(2,1)S(1)}, u32[]{:S(2)}, u32[]{:S(2)}) collective-permute-start(bf16[128,256]{1,0:T(8,128)(2,1)S(1)} %copy.131), channel_id=1, source_target_pairs={{8,0},{16,8},{24,16},{9,1},{17,9},{25,17},{10,2},{18,10},{26,18},{... | collective-permute-start | bytes 196616 | tf_op jit(solution)/shard_map/ppermute | solution.py:27
  183.5 12.6 %copy-start.18 = (bf16[4,64,8,128]{3,1,2,0:T(8,128)(2,1)}, bf16[4,64,8,128]{3,1,2,0:T(8,128)(2,1)S(1)}, u32[]{:S(2)}) copy-start(bf16[4,64,8,128]{3,1,2,0:T(8,128)(2,1)S(1)} %fusion.55) | copy-start | bytes 1572868
  183.6 7.1 %collective-permute-start.5 = (bf16[128,256]{0,1:T(8,128)(2,1)S(1)}, bf16[128,256]{0,1:T(8,128)(2,1)S(1)}, u32[]{:S(2)}, u32[]{:S(2)}) collective-permute-start(bf16[128,256]{0,1:T(8,128)(2,1)S(1)} %bitcast.454), channel_id=1, source_target_pairs={{8,0},{16,8},{24,16},{9,1},{17,9},{25,17},{10,2},{18,10},{26,18},{... | collective-permute-start | bytes 196616 | tf_op jit(solution)/shard_map/ppermute | solution.py:27
  186.8 9.4 %copy-start.23 = (bf16[128,256]{0,1:T(8,128)(2,1)}, bf16[128,256]{0,1:T(8,128)(2,1)S(1)}, u32[]{:S(2)}) copy-start(bf16[128,256]{0,1:T(8,128)(2,1)S(1)} %copy.134) | copy-start | bytes 196612
  190.7 6.3 %slice-start = ((s8[5898240]{0:T(1024)(128)(4,1)}), s8[4194304]{0:T(1024)(128)(4,1)S(1)}, s32[]{:S(2)}) async-start(s8[5898240]{0:T(1024)(128)(4,1)} %bitcast.420), calls=%async_computation.9 | async-start | bytes 8388608
  197.1 8.3 %copy-start.15 = (bf16[128,1440]{0,1:T(8,128)(2,1)}, bf16[128,1440]{0,1:T(8,128)(2,1)S(1)}, u32[]{:S(2)}) copy-start(bf16[128,1440]{0,1:T(8,128)(2,1)S(1)} %fusion.57) | copy-start | bytes 1105924
  210.9 158.6 %reduce-scatter.6.cloned.1.call-start = ((), (), s32[]{:S(2)}) async-start(), calls=%async_computation.4 | async-start | bytes 327680 | tf_op jit(solution)/shard_map/reduce_scatter | solution.py:370
  211.9 11.9 %copy-start.24 = (bf16[128,256]{0,1:T(8,128)(2,1)S(1)}, bf16[128,256]{0,1:T(8,128)(2,1)}, u32[]{:S(2)}) copy-start(bf16[128,256]{0,1:T(8,128)(2,1)} %copy-done.23) | copy-start | bytes 196612
  211.9 11.9 %copy-start.26 = (bf16[128,256]{0,1:T(8,128)(2,1)S(1)}, bf16[128,256]{0,1:T(8,128)(2,1)}, u32[]{:S(2)}) copy-start(bf16[128,256]{0,1:T(8,128)(2,1)} %copy-done.25) | copy-start | bytes 196612
  212.0 11.9 %copy-start.36 = (f32[128]{0:T(128)S(1)}, f32[128]{0:T(128)}, u32[]{:S(2)}) copy-start(f32[128]{0:T(128)} %copy-done.35) | copy-start | bytes 1540
  216.1 14.5 %copy-start.2 = (f32[512,256]{0,1:T(8,128)}, f32[512,256]{0,1:T(8,128)S(1)}, u32[]{:S(2)}) copy-start(f32[512,256]{0,1:T(8,128)S(1)} %get-tuple-element.1989) | copy-start | bytes 1572868
  216.1 14.0 %collective-permute-start.6 = (bf16[64,2048]{1,0:T(8,128)(2,1)}, bf16[64,2048]{1,0:T(8,128)(2,1)S(1)}, u32[]{:S(2)}, u32[]{:S(2)}) collective-permute-start(bf16[64,2048]{1,0:T(8,128)(2,1)} %get-tuple-element.1321), channel_id=1, source_target_pairs={{0,16},{8,24},{16,0},{24,8},{1,17},{9,25},{17,1},{25,9},{2,18},{10... | collective-permute-start | bytes 786440 | tf_op jit(solution)/shard_map/ppermute | solution.py:21
  252.0 96.0 %copy-start.38 = (u32[32]{0:T(128)S(1)}, u32[32]{0:T(128)}, u32[]{:S(2)}) copy-start(u32[32]{0:T(128)} %constant.418) | copy-start | bytes 388
  252.0 170.5 %all-reduce.6.cloned.1.call-start = ((), (), s32[]{:S(2)}) async-start(), calls=%async_computation.8 | async-start | bytes 3358720 | tf_op jit(solution)/shard_map/psum | solution.py:380
  346.7 2.6 collective-permute-start.8
  357.5 92.9 %reduce-scatter.8.cloned.1.call-start = ((), (), s32[]{:S(2)}) async-start(), calls=%async_computation.5 | async-start | bytes 327680 | tf_op jit(solution)/shard_map/reduce_scatter | solution.py:373
  358.9 9.7 %collective-permute-start.7 = (bf16[64,2048]{1,0:T(8,128)(2,1)S(1)}, bf16[64,2048]{1,0:T(8,128)(2,1)S(1)}, u32[]{:S(2)}, u32[]{:S(2)}) collective-permute-start(bf16[64,2048]{1,0:T(8,128)(2,1)S(1)} %copy.189), channel_id=1, source_target_pairs={{0,16},{8,24},{16,0},{24,8},{1,17},{9,25},{17,1},{25,9},{2,18},{10... | collective-permute-start | bytes 786440 | tf_op jit(solution)/shard_map/ppermute | solution.py:21
  (29 other events, 65.2 us)
Sparse Core Ops, SparseCore 0:
  9.6 64.6 all-gather.5
  75.9 73.1 all-gather.7
  211.0 81.8 reduce-scatter.9
  295.4 32.1 reduce-scatter.5
  357.6 64.9 all-reduce.5
  425.8 24.5 reduce-scatter.7
where the time goes:
time: 459 us; the launch traced here: 457 us
  waiting for transfers between devices  176 us (38%)
  blocking collectives  114 us (25%)
  matrix products  54 us (12%)
  local copies, waits for them, and re-layouts  43.9 us (10%)
  starting transfers between devices  24 us (5%)
  other arithmetic  23.9 us (5%)
  between operations  20.8 us (5%)
    unnamed x1, blocking collectives  94.5 us
    all_gather x1, waiting for transfers between devices, per_device(): lax.all_gather(w_qkv, 'fsdp', axis=0, tiled=True)  70 us
    psum x1, waiting for transfers between devices, per_device(): lax.psum(out_share, 'ctx').astype(jnp.float32)  51.7 us
    unnamed x79, local copies, waits for them, and re-layouts  25.7 us
    reduce_scatter x1, waiting for transfers between devices, per_device(): lax.psum_scatter(value_sums.astype(jnp.bfloat16), 'ctx', scatter_dimensio...  23.9 us
    ppermute x4, waiting for transfers between devices, partner_2(): return lax.ppermute(value, axis, pairs)  15.1 us
    ppermute x4, starting transfers between devices, partner_2(): return lax.ppermute(value, axis, pairs)  12.3 us
    ppermute x4, starting transfers between devices, from_behind(): lax.ppermute(value, axis, [(source, source + steps) for source in range(l...  10.2 us
  transfers between devices with their start and end apart: 15, of which 9 were waited for; matrix products, arithmetic and copies ran while one was open for 37% of the time, Pallas kernels for 0%

commit v1 on v0

v1 whole, which is shorter than its diff:
```python
import functools

import jax
import jax.numpy as jnp
from jax import lax
from jax.experimental import pallas as pl
from jax.experimental.pallas import tpu as pltpu
from jax.sharding import PartitionSpec as P

H = 32
KV = 4
DH = 64
BAND = 128


MASKED = -1e30
EPSILON = 1e-05


def from_behind(value, axis, steps):
    count = lax.axis_size(axis)
    leading, last = (max(0, -steps), min(count, count - steps))
    return lax.ppermute(value, axis, [(source, source + steps) for source in range(leading, last)])


def doc_table(lengths, seq_len):
    ends = jnp.cumsum(lengths)
    places = jnp.arange(seq_len, dtype=jnp.int32)
    before = places[:, None] >= ends[None, :]
    return jnp.sum(before.astype(jnp.int32), axis=1)


def attend_kernel(with_output, with_grads, *refs):
    refs = list(refs)
    allowed_ref, q_ref, k_ref, v_ref, v_t_ref = refs[:5]
    del refs[:5]
    if with_grads:
        k_t_ref, g_ref = refs[:2]
        del refs[:2]
    o_ref = refs.pop(0)
    if with_grads:
        dq_ref, dk_ref, dv_ref = refs
    allowed = allowed_ref[...] > 0.0
    keys, values, values_t = (k_ref[0], v_ref[0], v_t_ref[...])
    dk = jnp.zeros(keys.shape, jnp.float32)
    dv = jnp.zeros(keys.shape, jnp.float32)
    by_last = (((1,), (1,)), ((), ()))
    for head in range(H // KV):
        rows = slice(head * DH, (head + 1) * DH)
        query = q_ref[rows, :]
        scores = jnp.dot(keys, query, preferred_element_type=jnp.float32) * DH ** (-0.5)
        scores = jnp.where(allowed, scores, MASKED)
        row_max = jnp.max(scores, axis=0, keepdims=True)
        log_total = row_max + jnp.log(
            jnp.sum(jnp.exp(scores - row_max), axis=0, keepdims=True)
        )
        weights = jnp.where(allowed, jnp.exp(scores - log_total), 0.0)
        weights_bf = weights.astype(jnp.bfloat16)
        if with_output:
            output = jnp.dot(values_t, weights_bf, preferred_element_type=jnp.float32)
            output = output.astype(jnp.bfloat16)
            o_ref[rows, :] = output
        else:
            output = o_ref[rows, :]
        if with_grads:
            grad = g_ref[rows, :]
            correction = jnp.sum(
                grad.astype(jnp.float32) * output.astype(jnp.float32), axis=0, keepdims=True
            )
            grad_weights = jnp.dot(values, grad, preferred_element_type=jnp.float32)
            grad_scores = (weights * (grad_weights - correction)).astype(jnp.bfloat16)
            grad_q = jnp.dot(k_t_ref[...], grad_scores, preferred_element_type=jnp.float32)
            dq_ref[rows, :] = (grad_q * DH ** (-0.5)).astype(jnp.bfloat16)
            dk += lax.dot_general(grad_scores, query, by_last, preferred_element_type=jnp.float32)
            dv += lax.dot_general(weights_bf, grad, by_last, preferred_element_type=jnp.float32)
    if with_grads:
        dk_ref[0] = dk
        dv_ref[0] = dv


def by_head(rows):
    return rows.reshape(rows.shape[0], KV, DH).transpose(1, 0, 2)


def from_heads(heads):
    return heads.transpose(1, 0, 2).reshape(heads.shape[1], KV * DH)


def attend(allowed_t, query_t, keys, values, output_t=None, grad_t=None):
    columns, rows = allowed_t.shape
    with_output, with_grads = (output_t is None, grad_t is not None)
    group = pl.BlockSpec((query_t.shape[0] // KV, rows), lambda g: (g, 0))
    key_rows = pl.BlockSpec((1, columns, DH), lambda g: (g, 0, 0))
    key_columns = pl.BlockSpec((DH, columns), lambda g: (g, 0))
    args = [allowed_t, query_t, by_head(keys), by_head(values), values.T]
    in_specs = [pl.BlockSpec((columns, rows), lambda g: (0, 0)), group]
    in_specs += [key_rows, key_rows, key_columns]
    out_shape, out_specs = ([], [])
    wide = jax.ShapeDtypeStruct(query_t.shape, jnp.bfloat16)
    narrow = jax.ShapeDtypeStruct((KV, columns, DH), jnp.float32)
    if with_grads:
        args += [keys.T, grad_t]
        in_specs += [key_columns, group]
    if with_output:
        out_shape.append(wide)
        out_specs.append(group)
    else:
        args.append(output_t)
        in_specs.append(group)
    if with_grads:
        out_shape += [wide, narrow, narrow]
        out_specs += [group, key_rows, key_rows]
    return pl.pallas_call(
        functools.partial(attend_kernel, with_output, with_grads),
        grid=(KV,),
        out_shape=tuple(out_shape),
        in_specs=in_specs,
        out_specs=tuple(out_specs),
    )(*args)


MESH = pl.DeviceIdType.MESH


def remote(src, dst, send_sem, recv_sem, ctx, fsdp):
    return pltpu.make_async_remote_copy(
        src_ref=src,
        dst_ref=dst,
        send_sem=send_sem,
        recv_sem=recv_sem,
        device_id={"ctx": ctx, "fsdp": fsdp},
        device_id_type=MESH,
    )


def place():
    return (lax.axis_index("ctx"), lax.axis_index("fsdp"))


def shard_at(z, core, planes, offset):
    return 2 * lax.rem(z + offset, planes) + core


def greet(planes):
    c, f = place()
    z, core = (f // 2, lax.rem(f, 2))
    barrier = pltpu.get_barrier_semaphore()
    peers = [(c ^ 1, f), (c ^ 2, f), (c ^ 3, f), (c, f ^ 1)]
    peers += [(c, shard_at(z, core, planes, d)) for d in range(1, planes)]
    for ctx, fsdp in peers:
        pl.semaphore_signal(
            barrier, inc=1, device_id={"ctx": ctx, "fsdp": fsdp}, device_id_type=MESH
        )
    pl.semaphore_wait(barrier, len(peers))


def quarter_of(ref, weight, quarter):
    if weight == 0:
        size = ref.shape[0] // 4
        return ref.at[pl.ds(pl.multiple_of(quarter * size, 16), size), :]
    size = ref.shape[1] // 4
    return ref.at[:, pl.ds(pl.multiple_of(quarter * size, 128), size)]


def by_distance(planes):
    order = []
    for step in range(1, planes // 2 + 1):
        for d in (step, planes - step):
            if d not in order:
                order.append(d)
    return order


def gather_kernel(
    planes, wo, wq, kv, go, gq, gkv, send, recv_z, recv_x, recv_y, recv_d, recv_p, recv_kv, local
):
    c, f = place()
    z, core = (f // 2, lax.rem(f, 2))
    mine, full = ((wo, wq), (go, gq))
    rows = kv.shape[0]
    owns = [
        pltpu.make_async_copy(kv, gkv.at[pl.ds(pl.multiple_of(c * rows, 128), rows)], local),
        pltpu.make_async_copy(wo, go.at[f], local),
        pltpu.make_async_copy(wq, gq.at[f], local),
    ]
    for copy in owns:
        copy.start()
    greet(planes)
    started = []

    def push(*args):
        copy = remote(*args)
        copy.start()
        started.append(copy)

    def piece(weight, shard, quarter):
        return quarter_of(full[weight].at[shard], weight, quarter)

    def arrive(ref, sem):
        remote(ref, ref, send, sem, c ^ 1, f).wait_recv()

    kv_place = gkv.at[pl.ds(pl.multiple_of(c * rows, 128), rows)]
    for i, bit in enumerate((1, 2, 3)):
        push(kv, kv_place, send, recv_kv.at[i], c ^ bit, f)
    order = by_distance(planes)
    for weight in (0, 1):
        for d in order:
            push(
                quarter_of(mine[weight], weight, c),
                piece(weight, f, c),
                send,
                recv_z.at[weight, d],
                c,
                shard_at(z, core, planes, d),
            )
        push(mine[weight], full[weight].at[f], send, recv_p.at[weight, 0, 0], c, f ^ 1)
    steps = [(weight, d) for weight in (0, 1) for d in order]

    def to_partner(weight, d, shard, slot):
        part = piece(weight, shard, c ^ slot)
        push(part, part, send, recv_p.at[weight, d, slot], c, f ^ 1)

    def first(weight, d):
        shard = shard_at(z, core, planes, planes - d)
        part = piece(weight, shard, c)
        arrive(part, recv_z.at[weight, d])
        push(part, part, send, recv_x.at[weight, d], c ^ 1, f)
        push(part, part, send, recv_y.at[weight, d], c ^ 2, f)
        to_partner(weight, d, shard, 0)

    def second(weight, d):
        shard = shard_at(z, core, planes, planes - d)
        arrive(piece(weight, shard, c ^ 1), recv_x.at[weight, d])
        arrive(piece(weight, shard, c ^ 2), recv_y.at[weight, d])
        bit = jnp.where(core == weight, 1, 2)
        part = piece(weight, shard, c ^ bit)
        push(part, part, send, recv_d.at[weight, d], c ^ (3 - bit), f)
        to_partner(weight, d, shard, 1)
        to_partner(weight, d, shard, 2)

    def third(weight, d):
        shard = shard_at(z, core, planes, planes - d)
        arrive(piece(weight, shard, c ^ 3), recv_d.at[weight, d])
        to_partner(weight, d, shard, 3)

    count = len(steps)
    for i in range(count + 2):
        if i < count:
            first(*steps[i])
        if 0 <= i - 1 < count:
            second(*steps[i - 1])
        if 0 <= i - 2 < count:
            third(*steps[i - 2])
    for weight in (0, 1):
        arrive(full[weight].at[f ^ 1], recv_p.at[weight, 0, 0])
        for d in order:
            shard = shard_at(z, core, planes, planes - d) ^ 1
            for slot in range(4):
                arrive(piece(weight, shard, c ^ slot), recv_p.at[weight, d, slot])
    for i in range(3):
        arrive(kv_place, recv_kv.at[i])
    for copy in started:
        copy.wait_send()
    for copy in owns:
        copy.wait()


def gather_weights(w_out, w_qkv, kv):
    count = lax.axis_size("fsdp")
    planes = count // 2
    dma = pltpu.SemaphoreType.DMA
    anywhere = pl.BlockSpec(memory_space=pl.ANY)
    return pl.pallas_call(
        functools.partial(gather_kernel, planes),
        out_shape=(
            jax.ShapeDtypeStruct((count,) + w_out.shape, w_out.dtype),
            jax.ShapeDtypeStruct((count,) + w_qkv.shape, w_qkv.dtype),
            jax.ShapeDtypeStruct((4 * kv.shape[0], kv.shape[1]), kv.dtype),
        ),
        in_specs=[anywhere] * 3,
        out_specs=(anywhere,) * 3,
        scratch_shapes=[
            dma,
            dma((2, planes)),
            dma((2, planes)),
            dma((2, planes)),
            dma((2, planes)),
            dma((2, planes, 4)),
            dma((3,)),
            dma,
        ],
        compiler_params=pltpu.CompilerParams(collective_id=0, has_side_effects=True),
    )(w_out, w_qkv, kv)


def reduce_kernel(
    planes,
    att_t,
    norm_t,
    grad_mid,
    grad_proj,
    kv_sums,
    out_o,
    out_q,
    out_kv,
    a_o,
    a_q,
    s_o,
    s_q,
    p_o,
    p_q,
    r1_o,
    r1_q,
    r2_o,
    r2_q,
    rz_o,
    rz_q,
    from_kv,
    send,
    recv_p,
    recv_1,
    recv_2,
    recv_z,
    recv_f,
    recv_kv,
):
    c, f = place()
    z, core = (f // 2, lax.rem(f, 2))
    greet(planes)
    own, sent, from_p, from_1, from_2, from_z, result = (
        (a_o, a_q),
        (s_o, s_q),
        (p_o, p_q),
        (r1_o, r1_q),
        (r2_o, r2_q),
        (rz_o, rz_q),
        (out_o, out_q),
    )
    started = []

    def push(*args):
        copy = remote(*args)
        copy.start()
        started.append(copy)

    def arrive(ref, sem):
        remote(ref, ref, send, sem, c ^ 1, f).wait_recv()

    def term(weight, shard):
        if weight == 0:
            size = a_o.shape[1]
            left = att_t[pl.ds(pl.multiple_of(shard * size, size), size), :]
            right = grad_mid[...]
        else:
            left = norm_t[shard]
            right = grad_proj[...]
        return jnp.dot(left, right, preferred_element_type=jnp.float32).astype(jnp.bfloat16)

    def added(first, second):
        return (first.astype(jnp.float32) + second.astype(jnp.float32)).astype(jnp.bfloat16)

    rows = out_kv.shape[0]

    def kv_rows(index):
        return kv_sums.at[pl.ds(pl.multiple_of(index * rows, rows), rows), :]

    for slot in (3, 1, 2):
        push(
            kv_rows(c ^ slot), from_kv.at[slot], send, recv_kv.at[slot], c ^ slot, f
        )
    order = by_distance(planes)[::-1] + [0]
    steps = [(weight, d) for d in order for weight in (1, 0)]

    def bits(weight):
        bit = jnp.where(core == weight, 1, 2)
        return (bit, 3 - bit)

    def produce(weight, d):
        shard = shard_at(z, core, planes, d)
        sent[weight][d] = term(weight, shard ^ 1)
        push(sent[weight].at[d], from_p[weight].at[d], send, recv_p.at[weight, d], c, f ^ 1)
        own[weight][d] = term(weight, shard)

    def chip_sum(weight, d):
        arrive(from_p[weight].at[d], recv_p.at[weight, d])
        own[weight][d] = added(own[weight][d], from_p[weight][d])
        bit, other = bits(weight)
        for slot, quarter in ((1, c ^ 3), (0, c ^ bit)):
            push(
                quarter_of(own[weight].at[d], weight, quarter),
                from_1[weight].at[d, slot],
                send,
                recv_1.at[weight, d, slot],
                c ^ bit,
                f,
            )

    def pair_sum(weight, d):
        bit, other = bits(weight)
        for slot, quarter in ((1, c ^ other), (0, c)):
            arrive(from_1[weight].at[d, slot], recv_1.at[weight, d, slot])
            part = quarter_of(own[weight].at[d], weight, quarter)
            part[...] = added(part[...], from_1[weight][d, slot])
            if slot == 1:
                push(part, from_2[weight].at[d], send, recv_2.at[weight, d], c ^ other, f)

    def plane_sum(weight, d):
        arrive(from_2[weight].at[d], recv_2.at[weight, d])
        part = quarter_of(own[weight].at[d], weight, c)
        part[...] = added(part[...], from_2[weight][d])
        if d:
            push(
                part,
                from_z[weight].at[d],
                send,
                recv_z.at[weight, d],
                c,
                shard_at(z, core, planes, d),
            )

    def finish(weight):
        part = quarter_of(own[weight].at[0], weight, c)
        total = part[...].astype(jnp.float32)
        for d in range(1, planes):
            arrive(from_z[weight].at[d], recv_z.at[weight, d])
            total = total + from_z[weight][d].astype(jnp.float32)
        place_c = quarter_of(result[weight], weight, c)
        place_c[...] = total.astype(jnp.bfloat16)
        for slot in (3, 1, 2):
            push(place_c, place_c, send, recv_f.at[weight, slot], c ^ slot, f)

    stages = (produce, chip_sum, pair_sum, plane_sum)
    lags = (0, 2, 4, 6)
    count = len(steps)
    for i in range(count + lags[-1]):
        for stage, lag in zip(stages, lags):
            if 0 <= i - lag < count:
                stage(*steps[i - lag])
    kv_total = kv_rows(c)[...].astype(jnp.float32)
    for slot in (1, 2, 3):
        arrive(from_kv.at[slot], recv_kv.at[slot])
        kv_total += from_kv[slot].astype(jnp.float32)
    out_kv[...] = kv_total
    for weight in (1, 0):
        finish(weight)
    for weight in (1, 0):
        for slot in (3, 1, 2):
            arrive(quarter_of(result[weight], weight, c ^ slot), recv_f.at[weight, slot])
    for copy in started:
        copy.wait_send()


def reduce_weights(att_t, norm_t, grad_mid, grad_proj, kv_sums):
    count = lax.axis_size("fsdp")
    planes = count // 2
    dma = pltpu.SemaphoreType.DMA
    in_vmem = pl.BlockSpec(memory_space=pltpu.VMEM)
    bf = jnp.bfloat16
    o_shape = (att_t.shape[0] // count, grad_mid.shape[1])
    q_shape = (norm_t.shape[1], grad_proj.shape[1])
    o_part = (o_shape[0] // 4, o_shape[1])
    q_part = (q_shape[0], q_shape[1] // 4)
    scratch = []
    for lead, shapes in (
        ((planes,), (o_shape, q_shape)),
        ((planes,), (o_shape, q_shape)),
        ((planes,), (o_shape, q_shape)),
        ((planes, 2), (o_part, q_part)),
        ((planes,), (o_part, q_part)),
        ((planes,), (o_part, q_part)),
    ):
        scratch += [pltpu.VMEM(lead + shape, bf) for shape in shapes]
    kv_shape = (kv_sums.shape[0] // 4, kv_sums.shape[1])
    scratch.append(pltpu.VMEM((4,) + kv_shape, bf))
    return pl.pallas_call(
        functools.partial(reduce_kernel, planes),
        out_shape=(
            jax.ShapeDtypeStruct(o_shape, bf),
            jax.ShapeDtypeStruct(q_shape, bf),
            jax.ShapeDtypeStruct(kv_shape, jnp.float32),
        ),
        in_specs=[in_vmem] * 5,
        out_specs=(in_vmem,) * 3,
        scratch_shapes=scratch
        + [
            dma,
            dma((2, planes)),
            dma((2, planes, 2)),
            dma((2, planes)),
            dma((2, planes)),
            dma((2, 4)),
            dma((4,)),
        ],
        compiler_params=pltpu.CompilerParams(
            collective_id=1, has_side_effects=True, vmem_limit_bytes=60 * 2**20
        ),
    )(att_t, norm_t, grad_mid, grad_proj, kv_sums)


def per_device(query_a, key_a, value_a, resid_in, doc_lengths, w_out, w_qkv, grad_out, grad_resid):
    ctx_count = lax.axis_size("ctx")
    ctx_index = lax.axis_index("ctx")
    local_rows = query_a.shape[1]
    seq_len = local_rows * ctx_count
    band_len = BAND
    first_row = ctx_index * local_rows
    documents = doc_table(doc_lengths[0], seq_len)
    fsdp_count = lax.axis_size("fsdp")
    own_kernels = ctx_count == 4 and fsdp_count % 2 == 0 and w_out.shape[0] % 64 == 0
    if own_kernels:
        w_o3, w_b3, kv = gather_weights(
            w_out, w_qkv, jnp.concatenate([key_a[0], value_a[0]], axis=1)
        )
        w_o = w_o3.reshape(-1, w_out.shape[1])
        w_b = w_b3.reshape(-1, w_qkv.shape[1])
        keys, values = (kv[:, : KV * DH], kv[:, KV * DH :])
    else:
        w_o, w_b = (
            lax.all_gather(w_out, "fsdp", axis=0, tiled=True),
            lax.all_gather(w_qkv, "fsdp", axis=0, tiled=True),
        )
        keys, values = (
            lax.all_gather(key_a[0], "ctx", axis=0, tiled=True),
            lax.all_gather(value_a[0], "ctx", axis=0, tiled=True),
        )
    query_t = query_a[0].T
    row_docs = lax.dynamic_slice_in_dim(documents, first_row, local_rows)[None, :]
    row_places = (first_row + jnp.arange(local_rows, dtype=jnp.int32))[None, :]
    columns = jnp.arange(seq_len, dtype=jnp.int32)[:, None]
    allowed_t = ((documents[:, None] == row_docs) & (columns <= row_places)).astype(jnp.float32)
    (attended_t,) = attend(allowed_t, query_t, keys, values)
    attended = attended_t.T
    resid_mid = (
        resid_in[0].astype(jnp.float32) + jnp.dot(attended, w_o, preferred_element_type=jnp.float32)
    ).astype(jnp.bfloat16)
    resid_f = resid_mid.astype(jnp.float32)
    inverse_rms = lax.rsqrt(jnp.mean(resid_f * resid_f, axis=-1, keepdims=True) + EPSILON)
    normed = resid_f * inverse_rms
    normed_bf = normed.astype(jnp.bfloat16)
    projected = jnp.dot(normed_bf, w_b, preferred_element_type=jnp.float32).astype(jnp.bfloat16)
    query_b = projected[:, : H * DH]
    key_b = projected[:, H * DH : H * DH + KV * DH]
    value_b = projected[:, H * DH + KV * DH :]
    tails = from_behind(projected[:, H * DH :], "ctx", 1)
    tail_keys, tail_values = (tails[:, : KV * DH], tails[:, KV * DH :])
    keys_ext = jnp.concatenate([tail_keys, key_b], axis=0)
    values_ext = jnp.concatenate([tail_values, value_b], axis=0)
    doc_pad = jnp.concatenate([jnp.full((band_len,), -1, jnp.int32), documents])
    doc_ext = lax.dynamic_slice_in_dim(doc_pad, first_row, band_len + local_rows)
    ext_places = first_row - band_len + jnp.arange(band_len + local_rows, dtype=jnp.int32)
    ext_places = ext_places[:, None]
    band_t = (doc_ext[:, None] == row_docs) & (ext_places <= row_places)
    band_t = (band_t & (ext_places > row_places - band_len)).astype(jnp.float32)
    banded_t, grad_qb_t, key_heads, value_heads = attend(
        band_t, query_b.T, keys_ext, values_ext, None, grad_out[0].T
    )
    banded, grad_qb = (banded_t.T, grad_qb_t.T)
    key_ext_grad, value_ext_grad = (from_heads(key_heads), from_heads(value_heads))
    heads = jnp.concatenate([key_ext_grad[:band_len], value_ext_grad[:band_len]], axis=1)
    heads = from_behind(heads.astype(jnp.bfloat16), "ctx", -1).astype(jnp.float32)
    head_keys, head_values = (heads[:, : KV * DH], heads[:, KV * DH :])
    grad_kb = key_ext_grad[band_len:].at[local_rows - band_len :].add(head_keys)
    grad_vb = value_ext_grad[band_len:].at[local_rows - band_len :].add(head_values)
    grad_kb = (grad_kb * DH ** (-0.5)).astype(jnp.bfloat16)
    grad_vb = grad_vb.astype(jnp.bfloat16)
    grad_proj = jnp.concatenate([grad_qb, grad_kb, grad_vb], axis=1)
    grad_normed = jnp.dot(grad_proj, w_b.T, preferred_element_type=jnp.float32)
    middle = jnp.mean(grad_normed * normed, axis=-1, keepdims=True)
    grad_mid = (
        grad_resid[0].astype(jnp.float32) + inverse_rms * (grad_normed - normed * middle)
    ).astype(jnp.bfloat16)
    grad_attended = jnp.dot(grad_mid, w_o.T, preferred_element_type=jnp.float32).astype(
        jnp.bfloat16
    )
    grad_query_t, key_heads, value_heads = attend(
        allowed_t, query_t, keys, values, attended_t, grad_attended.T
    )
    grad_query = grad_query_t.T
    key_sums, value_sums = (from_heads(key_heads), from_heads(value_heads))
    if own_kernels:
        norm_t = normed_bf.T.reshape(fsdp_count, -1, local_rows)
        kv_sums = jnp.concatenate([key_sums, value_sums], axis=1).astype(jnp.bfloat16)
        out_share, qkv_share, own_kv = reduce_weights(
            attended_t, norm_t, grad_mid, grad_proj, kv_sums
        )
        own_keys, own_values = (own_kv[:, : KV * DH], own_kv[:, KV * DH :])
        grad_w_out, grad_w_qkv = (out_share.astype(jnp.float32), qkv_share.astype(jnp.float32))
    else:
        own_keys, own_values = (
            lax.psum_scatter(
                key_sums.astype(jnp.bfloat16), "ctx", scatter_dimension=0, tiled=True
            ).astype(jnp.float32),
            lax.psum_scatter(
                value_sums.astype(jnp.bfloat16), "ctx", scatter_dimension=0, tiled=True
            ).astype(jnp.float32),
        )
        piece = normed_bf
        qkv_share = lax.psum_scatter(
            jnp.einsum("tf,tc->fc", piece, grad_proj, preferred_element_type=jnp.float32).astype(
                jnp.bfloat16
            ),
            "fsdp",
            scatter_dimension=0,
            tiled=True,
        )
        piece = attended
        out_share = lax.psum_scatter(
            jnp.einsum("tf,tc->fc", piece, grad_mid, preferred_element_type=jnp.float32).astype(
                jnp.bfloat16
            ),
            "fsdp",
            scatter_dimension=0,
            tiled=True,
        )
        grad_w_out, grad_w_qkv = (
            lax.psum(out_share, "ctx").astype(jnp.float32),
            lax.psum(qkv_share, "ctx").astype(jnp.float32),
        )
    grad_key = (own_keys * DH ** (-0.5)).astype(jnp.bfloat16)
    grad_value = own_values.astype(jnp.bfloat16)
    return (
        banded[None],
        grad_mid[None],
        grad_query[None],
        grad_key[None],
        grad_value[None],
        grad_w_out,
        grad_w_qkv,
    )


def solution(mesh):
    in_specs = (
        P("fsdp", "ctx", None),
        P("fsdp", "ctx", None),
        P("fsdp", "ctx", None),
        P("fsdp", "ctx", None),
        P("fsdp", None),
        P("fsdp", None),
        P("fsdp", None),
        P("fsdp", "ctx", None),
        P("fsdp", "ctx", None),
    )
    out_specs = (
        P("fsdp", "ctx", None),
        P("fsdp", "ctx", None),
        P("fsdp", "ctx", None),
        P("fsdp", "ctx", None),
        P("fsdp", "ctx", None),
        P("fsdp", None),
        P("fsdp", None),
    )
    return jax.shard_map(
        per_device, mesh=mesh, in_specs=in_specs, out_specs=out_specs, check_vma=False
    )
```

time: 459 us -> 285 us (0.62)
  Pallas kernels: 0 us -> 210 us
  waiting for transfers between devices: 176 us -> 0.23 us
  blocking collectives: 114 us -> 0 us
  matrix products: 54 us -> 15.7 us
  starting transfers between devices: 24 us -> 2.77 us
  between operations: 20.8 us -> 1.01 us
  other arithmetic: 23.9 us -> 15.9 us
  local copies, waits for them, and re-layouts: 43.9 us -> 39 us
    pallas_call x0 -> x5, Pallas kernels: none -> 210 us  [the longest x1 93.8 us: reduce_weights(): pl.pallas_call(functools.partial(reduce_kernel, planes), out_shape=(jax.S...]
    unnamed x1 -> x0, blocking collectives: 94.5 us -> none
    all_gather x2 -> x0, waiting for transfers between devices: 79.2 us -> none  [the longest x1 70 us: per_device(): lax.all_gather(w_qkv, 'fsdp', axis=0, tiled=True)]
    psum x1 -> x0, waiting for transfers between devices: 51.7 us -> none  [per_device(): lax.psum(out_share, 'ctx').astype(jnp.float32)]
    dot_general x29 -> x0, matrix products: 38.4 us -> none  [the longest x3 7.45 us: add_values(): jnp.einsum('kgij,jkd->ikgd', weights, value_block, preferred_element_type...]
    reduce_scatter x3 -> x0, waiting for transfers between devices: 23.9 us -> none  [the longest x1 23.9 us: per_device(): lax.psum_scatter(value_sums.astype(jnp.bfloat16), 'ctx', scatter_dimensio...]
    all_gather x2 -> x0, blocking collectives: 19 us -> none  [the longest x1 9.81 us: per_device(): lax.all_gather(value_a[0], 'ctx', axis=0, tiled=True)]
    ppermute x4 -> x0, waiting for transfers between devices: 15.1 us -> none  [partner_2(): return lax.ppermute(value, axis, pairs)]
  transfers between devices with their start and end apart: 15 -> 2, of which waited for: 9 -> 1; matrix products, arithmetic and copies ran while one was open for 37% -> 4% of each run, Pallas kernels for 0% -> 0%
where the time goes in v1:
time: 285 us; the launch traced here: 284 us
  Pallas kernels  210 us (74%)
  local copies, waits for them, and re-layouts  39 us (14%)
  other arithmetic  15.9 us (6%)
  matrix products  15.7 us (6%)
    pallas_call x1, Pallas kernels, reduce_weights(): pl.pallas_call(functools.partial(reduce_kernel, planes), out_shape=(jax.S...  93.8 us
    pallas_call x1, Pallas kernels, gather_weights(): pl.pallas_call(functools.partial(gather_kernel, planes), out_shape=(jax.S...  67.9 us
    pallas_call x3, Pallas kernels, attend(): pl.pallas_call(functools.partial(attend_kernel, with_output, with_grads),...  48 us
    unnamed x37, local copies, waits for them, and re-layouts  14 us
    reshape x1, local copies, waits for them, and re-layouts, per_device(): w_b = w_b3.reshape(-1, w_qkv.shape[1])  7.11 us
  transfers between devices with their start and end apart: 2, of which 1 were waited for; matrix products, arithmetic and copies ran while one was open for 4% of the time, Pallas kernels for 0%

profile of v1, /device:TPU:0, one launch (start us, length us, event | category | flops | bytes accessed | tf_op | source)
XLA Modules:
  0.0 284.3 jit_solution(1404726211749528346)
XLA Ops:
  2.1 2.3 copy.78.wo
  4.3 1.5 pad_maximum_fusion.2.kv
  5.9 67.9 %shard_map.154 = (bf16[8,256,1440]{2,1,0:T(8,128)(2,1)}, bf16[8,180,2560]{2,1,0:T(8,128)(2,1)}, bf16[512,512]{1,0:T(8,128)(2,1)}) custom-call(bf16[256,1440]{1,0:T(8,128)(2,1)} %copy.78.wo, bf16[180,2560]{1,0:T(8,128)(2,1)} %wq.1, bf16[128,512]{1,0:T(8,128)(2,1)} %pad_maximum_fusion.2.kv), custom_call_target="tpu_custom_call" | custom-call | tf_op jit(solution)/shard_map/pallas_call | solution.py:273
  73.8 7.1 %reshape.163 = bf16[1440,2560]{1,0:T(8,128)(2,1)} reshape(bf16[8,180,2560]{2,1,0:T(8,128)(2,1)} %get-tuple-element.62) | data formatting | bytes 14745600 | tf_op jit(solution)/shard_map/reshape | solution.py:515
  81.0 1.0 copy.77
  82.0 1.0 copy.79
  83.0 2.1 slice_bitcast_fusion.2
  85.1 2.0 copy.80
  87.0 1.0 copy.82
  88.1 1.9 copy.76
  90.9 13.5 %shard_map.155.refs_7_.att_t = bf16[2048,128]{1,0:T(8,128)(2,1)} custom-call(f32[512,128]{1,0:T(8,128)} %fusion.4.refs_0_, bf16[2048,128]{1,0:T(8,128)(2,1)} %bitcast.76, bf16[4,512,64]{2,1,0:T(8,128)(2,1)} %bitcast.78, bf16[4,512,64]{2,1,0:T(8,128)(2,1)} %bitcast.80, bf16[256,512]{1,0:T(8,128)(2,1)} %get-tuple-element.99.refs_4_), custom_call_target="tpu_custom_call" | custom-call | tf_op jit(solution)/shard_map/pallas_call | solution.py:113
  104.4 4.2 %multiply_reduce_fusion.1 = (f32[128]{0:T(128)S(1)}, f32[128,1440]{1,0:T(8,128)S(1)}) fusion(bf16[2048,128]{1,0:T(8,128)(2,1)} %shard_map.155.refs_7_.att_t, bf16[2048,1440]{1,0:T(8,128)(2,1)} %bitcast.69, bf16[1,128,1440]{2,1,0:T(8,128)(2,1)} %copy.76), kind=kOutput, calls=%fused_computation.8 | convolution fusion | flops 756080512 | bytes 7528960 | tf_op jit(solution)/shard_map/dot_general | solution.py:534
  108.7 3.2 %convolution_convert_fusion = bf16[128,2560]{0,1:T(8,128)(2,1)S(1)} fusion(bf16[1440,2560]{1,0:T(8,128)(2,1)S(1)} %bitcast.68, f32[128,1440]{1,0:T(8,128)S(1)} %get-tuple-element.111, f32[128]{0:T(128)S(1)} %add_rsqrt_fusion), kind=kOutput, calls=%fused_computation | convolution fusion | flops 944414720 | bytes 8765952 | tf_op jit(solution)/shard_map/dot_general | solution.py:540
  111.9 1.3 collective-permute-start
  114.1 2.0 copy.87
  116.2 1.5 and_convert_fusion.refs_0_
  120.8 17.5 %shard_map.156 = (bf16[2048,128]{1,0:T(8,128)(2,1)}, bf16[2048,128]{1,0:T(8,128)(2,1)}, f32[4,256,64]{2,1,0:T(8,128)}, f32[4,256,64]{2,1,0:T(8,128)}) custom-call(f32[256,128]{1,0:T(8,128)} %and_convert_fusion.refs_0_, bf16[2048,128]{1,0:T(8,128)(2,1)} %slice_bitcast_fusion.refs_1_, bf16[4,256,64]{2,1,0:T(8,128)(2,1)} %bitcast.83, ...), custom_call_target="tpu_custom_call" | custom-call | tf_op jit(solution)/shard_map/pallas_call | solution.py:113
  139.4 1.0 slice.146
  140.6 1.5 collective-permute-start.1
  144.3 2.0 copy.105
  146.8 1.3 copy.89
  148.4 5.7 %fusion.13 = f32[128,1440]{1,0:T(8,128)S(1)} fusion(bf16[1440,2560]{1,0:T(8,128)(2,1)} %reshape.163, bf16[128,256]{1,0:T(8,128)(2,1)S(1)} %get-tuple-element.103, bf16[128,256]{1,0:T(8,128)(2,1)S(1)} %get-tuple-element.102, bf16[128,2048]{1,0:T(8,128)(2,1)S(1)} %bitcast.74), kind=kOutput, calls=%fused_computation.47 | convolution fusion | flops 945684480 | bytes 8765440 | tf_op jit(solution)/shard_map/dot_general | solution.py:567
  155.6 2.6 convolution_convert_fusion.1.refs_6_
  159.2 17.0 %shard_map.157 = (bf16[2048,128]{1,0:T(8,128)(2,1)}, f32[4,512,64]{2,1,0:T(8,128)}, f32[4,512,64]{2,1,0:T(8,128)}) custom-call(f32[512,128]{1,0:T(8,128)} %fusion.4.refs_0_, bf16[2048,128]{1,0:T(8,128)(2,1)} %bitcast.77, bf16[4,512,64]{2,1,0:T(8,128)(2,1)} %bitcast.79, bf16[4,512,64]{2,1,0:T(8,128)(2,1)} %bitcast.81, ...), custom_call_target="tpu_custom_call" | custom-call | tf_op jit(solution)/shard_map/pallas_call | solution.py:113
  176.2 1.4 convert_bitcast_fusion
  177.9 1.3 convert_bitcast_fusion.1
  180.4 93.8 %shard_map.158 = (bf16[256,1440]{1,0:T(8,128)(2,1)}, bf16[180,2560]{1,0:T(8,128)(2,1)}, f32[128,512]{1,0:T(8,128)}) custom-call(bf16[2048,128]{1,0:T(8,128)(2,1)} %shard_map.155.refs_7_.att_t, bf16[8,180,128]{2,1,0:T(8,128)(2,1)} %reshape.166.norm_t, bf16[128,1440]{1,0:T(8,128)(2,1)} %copy-done.2, bf16[128,2560]{1,0:T(8,128)(2,1)} %pad_maximum_fusion.grad_proj, ...), custom_call_target="tpu_custom_call" | custom-call | tf_op jit(solution)/shard_map/pallas_call | solution.py:475
  274.1 1.5 fusion.8
  275.7 1.5 fusion.9
  278.2 1.0 copy.107
  279.2 2.5 copy.108
  281.7 2.6 convert_element_type.79
  (74 shorter events, 15.5 us)
Async XLA Ops:
  1.2 88.9 %copy-start.8 = (s32[128]{0:T(128)}, s32[128]{0:T(128)S(1)}, u32[]{:S(2)}) copy-start(s32[128]{0:T(128)S(1)} %get-tuple-element.112) | copy-start | bytes 1540
  73.8 7.1 %copy-start.4 = (bf16[1,128,2048]{2,1,0:T(8,128)(2,1)S(1)}, bf16[1,128,2048]{2,1,0:T(8,128)(2,1)}, u32[]{:S(2)}) copy-start(bf16[1,128,2048]{2,1,0:T(8,128)(2,1)} %param.17) | copy-start | bytes 1572868
  73.8 8.1 %copy-start.6 = (bf16[512,512]{1,0:T(8,128)(2,1)S(1)}, bf16[512,512]{1,0:T(8,128)(2,1)}, u32[]{:S(2)}) copy-start(bf16[512,512]{1,0:T(8,128)(2,1)} %get-tuple-element.60) | copy-start | bytes 1572868
  83.0 25.7 %slice-start = ((s8[7372800]{0:T(1024)(128)(4,1)}), s8[3178496]{0:T(1024)(128)(4,1)S(1)}, s32[]{:S(2)}) async-start(s8[7372800]{0:T(1024)(128)(4,1)} %bitcast.67), calls=%async_computation | async-start | bytes 6356992
  90.0 18.6 %copy-start.9 = (s32[128]{0:T(128)}, s32[128]{0:T(128)S(1)}, u32[]{:S(2)}) copy-start(s32[128]{0:T(128)S(1)} %dynamic_slice.7) | copy-start | bytes 1540
  104.4 4.3 %slice-start.1 = ((s8[7372800]{0:T(1024)(128)(4,1)}), s8[4194304]{0:T(1024)(128)(4,1)S(1)}, s32[]{:S(2)}) async-start(s8[7372800]{0:T(1024)(128)(4,1)} %bitcast.67), calls=%async_computation.1 | async-start | bytes 8388608
  108.6 3.3 %copy-start = (f32[128,1440]{1,0:T(8,128)}, f32[128,1440]{1,0:T(8,128)S(1)}, u32[]{:S(2)}) copy-start(f32[128,1440]{1,0:T(8,128)S(1)} %get-tuple-element.111) | copy-start | bytes 2211844
  108.7 33.4 %copy-start.7 = (bf16[1,128,1440]{1,2,0:T(8,128)(2,1)S(1)}, bf16[1,128,1440]{1,2,0:T(8,128)(2,1)}, u32[]{:S(2)}) copy-start(bf16[1,128,1440]{1,2,0:T(8,128)(2,1)} %param.25) | copy-start | bytes 1105924
  111.9 5.8 %collective-permute-start = (bf16[128,512]{0,1:T(8,128)(2,1)S(1)}, bf16[128,512]{0,1:T(8,128)(2,1)S(1)}, u32[]{:S(2)}, u32[]{:S(2)}) collective-permute-start(bf16[128,512]{0,1:T(8,128)(2,1)S(1)} %slice.114), channel_id=1, source_target_pairs={{0,8},{8,16},{16,24},{1,9},{9,17},{17,25},{2,10},{10,18},{18,26},{... | collective-permute-start | bytes 393224 | tf_op jit(solution)/shard_map/ppermute | solution.py:23
  140.6 7.7 %collective-permute-start.1 = (bf16[128,512]{1,0:T(8,128)(2,1)S(1)}, bf16[128,512]{1,0:T(8,128)(2,1)S(1)}, u32[]{:S(2)}, u32[]{:S(2)}) collective-permute-start(bf16[128,512]{1,0:T(8,128)(2,1)S(1)} %pad_maximum_fusion.5), channel_id=1, source_target_pairs={{8,0},{16,8},{24,16},{9,1},{17,9},{25,17},{10,2},{18,10},{26,18},{... | collective-permute-start | bytes 393224 | tf_op jit(solution)/shard_map/ppermute | solution.py:23
  146.7 8.3 %copy-start.1 = (f32[128,1440]{1,0:T(8,128)S(1)}, f32[128,1440]{1,0:T(8,128)}, u32[]{:S(2)}) copy-start(f32[128,1440]{1,0:T(8,128)} %copy-done) | copy-start | bytes 2211844
  148.4 7.1 %slice-start.2 = ((s8[6291456]{0:T(1024)(128)(4,1)}), s8[4194304]{0:T(1024)(128)(4,1)S(1)}, s32[]{:S(2)}) async-start(s8[6291456]{0:T(1024)(128)(4,1)} %bitcast.70), calls=%async_computation.2 | async-start | bytes 8388608
  148.4 7.1 %slice-start.3 = ((s8[6291456]{0:T(1024)(128)(4,1)}), s8[2097152]{0:T(1024)(128)(4,1)S(1)}, s32[]{:S(2)}) async-start(s8[6291456]{0:T(1024)(128)(4,1)} %bitcast.70), calls=%async_computation.3 | async-start | bytes 4194304
  155.6 3.7 %copy-start.2 = (bf16[128,1440]{1,0:T(8,128)(2,1)}, bf16[128,1440]{1,0:T(8,128)(2,1)S(1)}, u32[]{:S(2)}) copy-start(bf16[128,1440]{1,0:T(8,128)(2,1)S(1)} %fusion.2.grad_mid) | copy-start | bytes 1105924
  159.2 118.0 %copy-start.3 = (bf16[128,1440]{1,0:T(8,128)(2,1)S(1)}, bf16[128,1440]{1,0:T(8,128)(2,1)}, u32[]{:S(2)}) copy-start(bf16[128,1440]{1,0:T(8,128)(2,1)} %copy-done.2) | copy-start | bytes 1105924
  176.2 101.9 %copy-start.5 = (bf16[2048,128]{1,0:T(8,128)(2,1)S(1)}, bf16[2048,128]{1,0:T(8,128)(2,1)}, u32[]{:S(2)}) copy-start(bf16[2048,128]{1,0:T(8,128)(2,1)} %get-tuple-element.67) | copy-start | bytes 1572868
